TPU v7x, 32 devices: a whole 2x2x4 slice. The times are simulated.
32 devices in a mesh: unit: 2 (over y), row: 4 (over x, core), col: 4 (over z).
Axes of the slice: x: 2, y: 2, z: 4, core: 2. Of those that a mesh axis runs over, the one named last changes fastest.
Arguments:
- tracer: float32 [4, 32, 64, 64], P('unit', None, 'row', 'col'), parts along dimension 0, may hold values from -6 to 6
- symbol_x: float32 [32], replicated, may hold values from 0.3 to 3
- symbol_y: float32 [64], replicated, may hold values from 0.3 to 3
- symbol_z: float32 [64], replicated, may hold values from 0.3 to 3
Outputs:
- smoothed: float32 [4, 32, 64, 64], P('unit', None, 'row', 'col'), parts along dimension 0
There are 2 independent parts, one for each index of `unit`. A program takes and returns all parts, laid end to end along the dimension named above; an argument that names none is the same for every part. Nothing has to cross between parts.
All inputs are finite; a program needn't handle non-finite values.
Results may differ from a plain program's by a relative error of at most 0.0003.
Values sent between devices are 32-bit elements.
A program may use at most 64 MiB of HBM per device.

v0:
```python
import jax
import jax.numpy as jnp
from jax import lax
from jax.sharding import PartitionSpec as P


def mode_table(count):
    rank = jnp.arange(count)
    angle = (
        jnp.pi
        / (4 * count)
        * ((2 * rank[:, None] + 1) * (2 * rank[None, :] + 1) % (8 * count)).astype(jnp.float32)
    )
    return jnp.cos(angle) * (2.0 / count) ** 0.5


def to_modes(values, dim):
    moved = jnp.tensordot(
        values, mode_table(values.shape[dim]), axes=([dim], [0]), precision=lax.Precision.HIGHEST
    )
    return jnp.moveaxis(moved, -1, dim)


def shards(tracer, symbol_x, symbol_y, symbol_z):

    def forward_part(part_values):
        part_values = to_modes(part_values, 1)
        part_values = lax.all_to_all(part_values, "row", split_axis=1, concat_axis=2, tiled=True)
        part_values = to_modes(part_values, 2)
        part_values = lax.all_to_all(part_values, "col", split_axis=2, concat_axis=3, tiled=True)
        return to_modes(part_values, 3)

    def backward_part(part_values):
        part_values = to_modes(part_values, 3)
        part_values = lax.all_to_all(part_values, "col", split_axis=3, concat_axis=2, tiled=True)
        part_values = to_modes(part_values, 2)
        part_values = lax.all_to_all(part_values, "row", split_axis=2, concat_axis=1, tiled=True)
        return to_modes(part_values, 1)

    block_values = forward_part(tracer)
    share_x = block_values.shape[1]
    part_x = lax.dynamic_slice_in_dim(symbol_x, lax.axis_index("row") * share_x, share_x)
    share_y = block_values.shape[2]
    part_y = lax.dynamic_slice_in_dim(symbol_y, lax.axis_index("col") * share_y, share_y)
    symbol = part_x[:, None, None] + part_y[None, :, None] + symbol_z[None, None, :]
    block_values = block_values * lax.rsqrt(symbol)
    block_values = backward_part(block_values)
    return block_values


def solution(mesh):
    in_specs = (P("unit", None, "row", "col"), P(), P(), P())
    out_specs = P("unit", None, "row", "col")
    return jax.shard_map(shards, mesh=mesh, in_specs=in_specs, out_specs=out_specs, check_vma=False)
```

profile of v0, /device:TPU:0, one launch (start us, length us, event | category | flops | bytes accessed | tf_op | source)
XLA Modules:
  0.0 49.6 jit_solution(17201556135171199942)
XLA Ops:
  0.0 0.0 copy-start
  0.0 0.9 %copy-done = f32[2,32,16,16]{1,3,2,0:T(8,128)S(1)} copy-done((f32[2,32,16,16]{1,3,2,0:T(8,128)S(1)}, f32[2,32,16,16]{1,3,2,0:T(8,128)}, u32[]{:S(2)}) %copy-start) | copy-done | bytes 65560
  1.0 0.5 %fusion.47 = f32[32,512]{0,1:S(1)} fusion(f32[32,512]{0,1:T(8,128)S(1)} %bitcast.57, s32[32]{0:T(128)S(1)} %multiply_add_fusion.1), kind=kOutput, calls=%fused_computation.59 | convolution fusion | flops 6306816 | bytes 131200
  1.5 0.5 copy.14
  1.9 0.9 %reshape.67 = f32[4,1,4096]{2,1,0:T(1,128)} reshape(f32[32,2,16,16]{3,2,1,0:T(8,128)S(1)} %bitcast.61) | data formatting | bytes 131072
  2.8 4.2 %all-to-all-start = ((f32[4,1,4096]{2,1,0:T(1,128)}), f32[4,1,4096]{2,1,0:T(1,128)S(1)}, u32[]{:S(2)}, u32[]{:S(2)}) async-start(f32[4,1,4096]{2,1,0:T(1,128)} %reshape.67), calls=%async_computation | async-start | bytes 131072 | tf_op jit(solution)/shard_map/all_to_all | solution.py:28
  7.0 0.0 copy-start.2
  7.0 0.7 %copy-done.2 = f32[64]{0:T(128)S(1)} copy-done((f32[64]{0:T(128)S(1)}, f32[64]{0:T(128)}, u32[]{:S(2)}) %copy-start.2) | copy-done | bytes 280
  7.7 0.1 dynamic_slice.7
  7.8 0.0 copy-start.3
  7.8 0.7 %copy-done.3 = f32[32]{0:T(128)S(1)} copy-done((f32[32]{0:T(128)S(1)}, f32[32]{0:T(128)}, u32[]{:S(2)}) %copy-start.3) | copy-done | bytes 152
  8.4 0.1 dynamic_slice.6
  8.5 0.1 broadcast_add_fusion
  8.6 2.6 %all-to-all-done = f32[4,1,4096]{2,1,0:T(1,128)S(1)} async-done(((f32[4,1,4096]{2,1,0:T(1,128)}), f32[4,1,4096]{2,1,0:T(1,128)S(1)}, u32[]{:S(2)}, u32[]{:S(2)}) %all-to-all-start) | async-done | bytes 65568 | tf_op jit(solution)/shard_map/all_to_all | solution.py:28
  11.2 0.6 %broadcast.193 = f32[]{:T(128)} broadcast(f32[]{:T(128)} %constant.155), dimensions={} | broadcast | bytes 8 | tf_op jit(solution)/shard_map/all_to_all | solution.py:28
  11.8 0.9 %reduce = f32[4,4096]{1,0:T(4,128)S(1)} reduce(f32[4,1,4096]{2,1,0:T(1,128)S(1)} %all-to-all-done, f32[]{:T(128)} %broadcast.193), dimensions={1}, to_apply=%all_to_all.52.reduce_sub_computation | reduce | bytes 131076 | tf_op jit(solution)/shard_map/all_to_all | solution.py:28
  12.6 0.2 reshape.68
  12.8 0.2 copy.16
  13.1 0.3 all_to_all.55
  13.3 0.5 convolution_bitcast_fusion.2
  13.8 0.3 copy.17
  14.1 0.9 %reshape.69 = f32[4,1,4096]{2,1,0:T(1,128)} reshape(f32[64,2,8,16]{3,2,1,0:T(8,128)S(1)} %bitcast.58) | data formatting | bytes 131072
  14.9 0.0 copy-start.1
  14.9 5.5 %all-to-all-start.1 = ((f32[4,1,4096]{2,1,0:T(1,128)}), f32[4,1,4096]{2,1,0:T(1,128)S(1)}, u32[]{:S(2)}, u32[]{:S(2)}) async-start(f32[4,1,4096]{2,1,0:T(1,128)} %reshape.69), calls=%async_computation.1 | async-start | bytes 131072 | tf_op jit(solution)/shard_map/all_to_all | solution.py:30
  20.4 0.0 copy-done.1
  20.4 0.1 add_rsqrt_fusion
  20.5 5.6 %all-to-all-done.1 = f32[4,1,4096]{2,1,0:T(1,128)S(1)} async-done(((f32[4,1,4096]{2,1,0:T(1,128)}), f32[4,1,4096]{2,1,0:T(1,128)S(1)}, u32[]{:S(2)}, u32[]{:S(2)}) %all-to-all-start.1) | async-done | bytes 65568 | tf_op jit(solution)/shard_map/all_to_all | solution.py:30
  26.2 0.9 %reduce.1 = f32[4,4096]{1,0:T(4,128)S(1)} reduce(f32[4,1,4096]{2,1,0:T(1,128)S(1)} %all-to-all-done.1, f32[]{:T(128)} %broadcast.193), dimensions={1}, to_apply=%all_to_all.56.reduce_sub_computation | reduce | bytes 131076 | tf_op jit(solution)/shard_map/all_to_all | solution.py:30
  27.0 0.2 reshape.70
  27.2 0.3 copy.32
  27.6 0.3 all_to_all.59
  27.8 0.5 convolution_multiply_fusion
  28.3 0.4 fusion.8
  28.8 0.3 copy.19
  29.1 0.2 reshape.71
  29.3 8.1 %all_to_all.72 = f32[4,1,4096]{2,1,0:T(1,128)S(1)} all-to-all(f32[4,1,4096]{2,1,0:T(1,128)S(1)} %reshape.71), channel_id=1, replica_groups=mesh['unit'=2,'row'=4,'col'=4] {'col'}, dimensions={0} | all-to-all | bytes 131072 | tf_op jit(solution)/shard_map/all_to_all | solution.py:35
  37.4 0.9 %reduce.2 = f32[4,4096]{1,0:T(4,128)S(1)} reduce(f32[4,1,4096]{2,1,0:T(1,128)S(1)} %all_to_all.72, f32[]{:T(128)} %broadcast.193), dimensions={1}, to_apply=%all_to_all.60.reduce_sub_computation | reduce | bytes 131076 | tf_op jit(solution)/shard_map/all_to_all | solution.py:35
  38.3 0.2 reshape.72
  38.5 0.3 copy.31
  38.8 0.3 all_to_all.63
  39.1 0.5 convolution_bitcast_fusion.1
  39.5 0.3 copy.21
  39.8 0.2 reshape.73
  40.1 6.5 %all_to_all.73 = f32[4,1,4096]{2,1,0:T(1,128)S(1)} all-to-all(f32[4,1,4096]{2,1,0:T(1,128)S(1)} %reshape.73), channel_id=1, replica_groups=mesh['unit'=2,'row'=4,'col'=4] {'row'}, dimensions={0} | all-to-all | bytes 131072 | tf_op jit(solution)/shard_map/all_to_all | solution.py:37
  46.5 0.9 %reduce.3 = f32[4,4096]{1,0:T(4,128)S(1)} reduce(f32[4,1,4096]{2,1,0:T(1,128)S(1)} %all_to_all.73, f32[]{:T(128)} %broadcast.193), dimensions={1}, to_apply=%all_to_all.64.reduce_sub_computation | reduce | bytes 131076 | tf_op jit(solution)/shard_map/all_to_all | solution.py:37
  47.4 0.2 reshape.74
  47.6 0.2 copy.22
  47.8 1.8 %convolution_bitcast_fusion = f32[2,32,16,16]{1,3,2,0:T(8,128)} fusion(f32[2,32,16,16]{3,2,1,0:T(8,128)S(1)} %bitcast.64, s32[32]{0:T(128)S(1)} %multiply_add_fusion.1), kind=kOutput, calls=%fused_computation | convolution fusion | flops 6306816 | bytes 131200 | tf_op jit(solution)/shard_map/dot_general | solution.py:18
  (2 shorter events, 0.0 us)
Async XLA Ops:
  0.0 1.0 %copy-start = (f32[2,32,16,16]{1,3,2,0:T(8,128)S(1)}, f32[2,32,16,16]{1,3,2,0:T(8,128)}, u32[]{:S(2)}) copy-start(f32[2,32,16,16]{1,3,2,0:T(8,128)} %param.4) | copy-start | bytes 196612
  2.8 8.4 %all-to-all-start = ((f32[4,1,4096]{2,1,0:T(1,128)}), f32[4,1,4096]{2,1,0:T(1,128)S(1)}, u32[]{:S(2)}, u32[]{:S(2)}) async-start(f32[4,1,4096]{2,1,0:T(1,128)} %reshape.67), calls=%async_computation | async-start | bytes 131072 | tf_op jit(solution)/shard_map/all_to_all | solution.py:28
  7.0 0.7 %copy-start.2 = (f32[64]{0:T(128)S(1)}, f32[64]{0:T(128)}, u32[]{:S(2)}) copy-start(f32[64]{0:T(128)} %param.6) | copy-start | bytes 772
  7.8 0.7 %copy-start.3 = (f32[32]{0:T(128)S(1)}, f32[32]{0:T(128)}, u32[]{:S(2)}) copy-start(f32[32]{0:T(128)} %param.5) | copy-start | bytes 388
  14.9 5.5 %copy-start.1 = (f32[64]{0:T(128)S(1)}, f32[64]{0:T(128)}, u32[]{:S(2)}) copy-start(f32[64]{0:T(128)} %param.7) | copy-start | bytes 772
  14.9 11.2 %all-to-all-start.1 = ((f32[4,1,4096]{2,1,0:T(1,128)}), f32[4,1,4096]{2,1,0:T(1,128)S(1)}, u32[]{:S(2)}, u32[]{:S(2)}) async-start(f32[4,1,4096]{2,1,0:T(1,128)} %reshape.69), calls=%async_computation.1 | async-start | bytes 131072 | tf_op jit(solution)/shard_map/all_to_all | solution.py:30
where the time goes:
time: 50.1 us; the launch traced here: 49.6 us
  blocking collectives  14.6 us (29%)
  starting transfers between devices  9.74 us (19%)
  local copies, waits for them, and re-layouts  9.15 us (18%)
  waiting for transfers between devices  8.23 us (16%)
  matrix products  4.09 us (8%)
  other arithmetic  3.59 us (7%)
    all_to_all x1, blocking collectives, backward_part(): lax.all_to_all(part_values, 'col', split_axis=3, concat_axis=2, tiled=True)  8.11 us
    all_to_all x1, blocking collectives, backward_part(): lax.all_to_all(part_values, 'row', split_axis=2, concat_axis=1, tiled=True)  6.49 us
    all_to_all x1, waiting for transfers between devices, forward_part(): lax.all_to_all(part_values, 'col', split_axis=2, concat_axis=3, tiled=True)  5.65 us
    all_to_all x1, starting transfers between devices, forward_part(): lax.all_to_all(part_values, 'col', split_axis=2, concat_axis=3, tiled=True)  5.5 us
    unnamed x16, local copies, waits for them, and re-layouts  5.27 us
    all_to_all x1, starting transfers between devices, forward_part(): lax.all_to_all(part_values, 'row', split_axis=1, concat_axis=2, tiled=True)  4.23 us
    dot_general x5, matrix products, to_modes(): jnp.tensordot(values, mode_table(values.shape[dim]), axes=([dim], [0]), p...  3.59 us
    all_to_all x1, waiting for transfers between devices, forward_part(): lax.all_to_all(part_values, 'row', split_axis=1, concat_axis=2, tiled=True)  2.58 us
  transfers between devices with their start and end apart: 2, of which 2 were waited for; matrix products, arithmetic and copies ran while one was open for 1% of the time, Pallas kernels for 0%

commit v1 on v0

--- a/solution.py
+++ b/solution.py
@@ -2,6 +2,21 @@
 import jax.numpy as jnp
 from jax import lax
 from jax.sharding import PartitionSpec as P
+
+
+def ends_register(inputs, row_dim, x_in):
+    arr_now, y = (inputs.shape[:row_dim], inputs.shape[row_dim + 1 :])
+    return jnp.moveaxis(inputs.reshape(*arr_now, x_in, -1, *y), row_dim, 0)
+
+
+def post_slot_now(vec, array_axis):
+    vec = jnp.moveaxis(vec, 0, array_axis)
+    value_now = vec.shape
+    return vec.reshape(
+        *value_now[:array_axis],
+        value_now[array_axis] * value_now[array_axis + 1],
+        *value_now[array_axis + 2 :]
+    )
 
 
 def mode_table(count):
@@ -24,10 +39,26 @@
 def shards(tracer, symbol_x, symbol_y, symbol_z):
 
     def forward_part(part_values):
+
+        def numbers_supply_all(shard_in, bus_axis, message, unit):
+            carry, opened = (lax.axis_size(bus_axis), lax.axis_index(bus_axis))
+            block_last = ends_register(unit, message, carry)
+            local_now = block_last
+            for q in range(1, carry):
+                f_now, reply = ((opened + q) % carry, (opened - q) % carry)
+                answer = lax.dynamic_index_in_dim(block_last, f_now, 0)
+                arr_out = lax.ppermute(
+                    answer,
+                    axis_name=bus_axis,
+                    perm=[(tick, (tick + q) % carry) for tick in range(carry)],
+                )
+                local_now = lax.dynamic_update_slice_in_dim(local_now, arr_out, reply, axis=0)
+            return post_slot_now(local_now, shard_in)
+
         part_values = to_modes(part_values, 1)
         part_values = lax.all_to_all(part_values, "row", split_axis=1, concat_axis=2, tiled=True)
         part_values = to_modes(part_values, 2)
-        part_values = lax.all_to_all(part_values, "col", split_axis=2, concat_axis=3, tiled=True)
+        part_values = numbers_supply_all(3, "col", 2, part_values)
         return to_modes(part_values, 3)
 
     def backward_part(part_values):

time: 50.1 us -> 59 us (1.18)
  local copies, waits for them, and re-layouts: 9.15 us -> 17 us
  blocking collectives: 14.6 us -> 18 us
  waiting for transfers between devices: 8.23 us -> 6.21 us
  other arithmetic: 3.59 us -> 2.61 us
  starting transfers between devices: 9.74 us -> 10.4 us
    dynamic_update_slice x0 -> x3, local copies, waits for them, and re-layouts: none -> 8.42 us  [numbers_supply_all(): lax.dynamic_update_slice_in_dim(local_now, arr_out, reply, axis=0)]
    ppermute x0 -> x3, starting transfers between devices: none -> 6.18 us  [numbers_supply_all(): lax.ppermute(answer, axis_name=bus_axis, perm=[(tick, (tick + q) % carry)...]
    all_to_all x1 -> x0, waiting for transfers between devices: 5.65 us -> none  [forward_part(): lax.all_to_all(part_values, 'col', split_axis=2, concat_axis=3, tiled=True)]
    all_to_all x1 -> x0, starting transfers between devices: 5.5 us -> none  [forward_part(): lax.all_to_all(part_values, 'col', split_axis=2, concat_axis=3, tiled=True)]
    ppermute x0 -> x3, waiting for transfers between devices: none -> 3.63 us  [numbers_supply_all(): lax.ppermute(answer, axis_name=bus_axis, perm=[(tick, (tick + q) % carry)...]
    all_to_all x1, blocking collectives: 8.11 us -> 11.6 us  [backward_part(): lax.all_to_all(part_values, 'col', split_axis=3, concat_axis=2, tiled=True)]
    unnamed x16 -> x14, local copies, waits for them, and re-layouts: 5.27 us -> 4.2 us
    all_to_all x1 -> x0, other arithmetic: 0.86 us -> none  [forward_part(): lax.all_to_all(part_values, 'col', split_axis=2, concat_axis=3, tiled=True)]
  transfers between devices with their start and end apart: 2 -> 4, of which waited for: 2 -> 3; matrix products, arithmetic and copies ran while one was open for 1% -> 11% of each run, Pallas kernels for 0% -> 0%
where the time goes in v1:
time: 59 us; the launch traced here: 58.6 us
  blocking collectives  18 us (31%)
  local copies, waits for them, and re-layouts  17 us (29%)
  starting transfers between devices  10.4 us (18%)
  waiting for transfers between devices  6.21 us (11%)
  matrix products  4.09 us (7%)
  other arithmetic  2.61 us (4%)
    all_to_all x1, blocking collectives, backward_part(): lax.all_to_all(part_values, 'col', split_axis=3, concat_axis=2, tiled=True)  11.6 us
    dynamic_update_slice x3, local copies, waits for them, and re-layouts, numbers_supply_all(): lax.dynamic_update_slice_in_dim(local_now, arr_out, reply, axis=0)  8.42 us
    all_to_all x1, blocking collectives, backward_part(): lax.all_to_all(part_values, 'row', split_axis=2, concat_axis=1, tiled=True)  6.49 us
    ppermute x3, starting transfers between devices, numbers_supply_all(): lax.ppermute(answer, axis_name=bus_axis, perm=[(tick, (tick + q) % carry)...  6.18 us
    all_to_all x1, starting transfers between devices, forward_part(): lax.all_to_all(part_values, 'row', split_axis=1, concat_axis=2, tiled=True)  4.23 us
    unnamed x14, local copies, waits for them, and re-layouts  4.2 us
    ppermute x3, waiting for transfers between devices, numbers_supply_all(): lax.ppermute(answer, axis_name=bus_axis, perm=[(tick, (tick + q) % carry)...  3.63 us
    dot_general x5, matrix products, to_modes(): jnp.tensordot(values, mode_table(values.shape[dim]), axes=([dim], [0]), p...  3.59 us
  transfers between devices with their start and end apart: 4, of which 3 were waited for; matrix products, arithmetic and copies ran while one was open for 11% of the time, Pallas kernels for 0%

profile of v1, /device:TPU:0, one launch (start us, length us, event | category | flops | bytes accessed | tf_op | source)
XLA Modules:
  0.0 58.6 jit_solution(1823772524335928814)
XLA Ops:
  0.0 0.0 copy-start
  0.0 0.9 %copy-done = f32[2,32,16,16]{1,3,2,0:T(8,128)S(1)} copy-done((f32[2,32,16,16]{1,3,2,0:T(8,128)S(1)}, f32[2,32,16,16]{1,3,2,0:T(8,128)}, u32[]{:S(2)}) %copy-start) | copy-done | bytes 65560
  1.0 0.5 fusion.47
  1.5 0.5 copy.17
  1.9 0.9 %reshape.78 = f32[4,1,4096]{2,1,0:T(1,128)} reshape(f32[32,2,16,16]{3,2,1,0:T(8,128)S(1)} %bitcast.65) | data formatting | bytes 131072
  2.8 4.2 %all-to-all-start = ((f32[4,1,4096]{2,1,0:T(1,128)}), f32[4,1,4096]{2,1,0:T(1,128)S(1)}, u32[]{:S(2)}, u32[]{:S(2)}) async-start(f32[4,1,4096]{2,1,0:T(1,128)} %reshape.78), calls=%async_computation | async-start | bytes 131072 | tf_op jit(solution)/shard_map/all_to_all | solution.py:59
  7.0 0.0 copy-start.2
  7.0 0.7 %copy-done.2 = f32[64]{0:T(128)S(1)} copy-done((f32[64]{0:T(128)S(1)}, f32[64]{0:T(128)}, u32[]{:S(2)}) %copy-start.2) | copy-done | bytes 280
  7.7 0.1 dynamic_slice.20
  7.8 0.0 copy-start.3
  7.8 0.7 %copy-done.3 = f32[32]{0:T(128)S(1)} copy-done((f32[32]{0:T(128)S(1)}, f32[32]{0:T(128)}, u32[]{:S(2)}) %copy-start.3) | copy-done | bytes 152
  8.4 0.1 dynamic_slice.19
  8.5 0.1 broadcast_add_fusion
  8.6 2.6 %all-to-all-done = f32[4,1,4096]{2,1,0:T(1,128)S(1)} async-done(((f32[4,1,4096]{2,1,0:T(1,128)}), f32[4,1,4096]{2,1,0:T(1,128)S(1)}, u32[]{:S(2)}, u32[]{:S(2)}) %all-to-all-start) | async-done | bytes 65568 | tf_op jit(solution)/shard_map/all_to_all | solution.py:59
  11.2 0.5 broadcast.199
  11.7 0.8 %reduce = f32[4,4096]{1,0:T(4,128)S(1)} reduce(f32[4,1,4096]{2,1,0:T(1,128)S(1)} %all-to-all-done, f32[]{:T(128)} %broadcast.199), dimensions={1}, to_apply=%all_to_all.39.reduce_sub_computation | reduce | bytes 131076 | tf_op jit(solution)/shard_map/all_to_all | solution.py:59
  12.5 0.2 reshape.79
  12.7 0.2 copy.19
  12.9 0.3 all_to_all.42
  13.2 0.5 convolution_bitcast_fusion.2
  13.7 0.3 reshape.72
  13.9 0.4 constant_dynamic-slice_fusion
  14.3 0.1 copy.21
  14.4 2.1 %collective-permute-start = (f32[1,2,8,16,16]{4,0,3,2,1:T(1,128)S(1)}, f32[1,2,8,16,16]{4,0,3,2,1:T(1,128)S(1)}, u32[]{:S(2)}, u32[]{:S(2)}) collective-permute-start(f32[1,2,8,16,16]{4,0,3,2,1:T(1,128)S(1)} %bitcast.74), channel_id=1, source_target_pairs={{0,1},{1,2},{2,3},{3,0},{4,5},{5,6},{6,7},{7,4},{8,9},{9,10},{10,1... | collective-permute-start | bytes 49160 | tf_op jit(solution)/shard_map/ppermute | solution.py:50
  16.6 0.1 copy.22
  16.6 2.7 %collective-permute-start.1 = (f32[1,2,8,16,16]{4,0,3,2,1:T(1,128)S(1)}, f32[1,2,8,16,16]{4,0,3,2,1:T(1,128)S(1)}, u32[]{:S(2)}, u32[]{:S(2)}) collective-permute-start(f32[1,2,8,16,16]{4,0,3,2,1:T(1,128)S(1)} %bitcast.73), channel_id=1, source_target_pairs={{0,2},{1,3},{2,0},{3,1},{4,6},{5,7},{6,4},{7,5},{8,10},{9,11},{10,... | collective-permute-start | bytes 49160 | tf_op jit(solution)/shard_map/ppermute | solution.py:50
  19.3 0.1 copy.23
  19.4 0.0 copy-start.1
  19.4 1.4 %collective-permute-start.2 = (f32[1,2,8,16,16]{4,0,3,2,1:T(1,128)S(1)}, f32[1,2,8,16,16]{4,0,3,2,1:T(1,128)S(1)}, u32[]{:S(2)}, u32[]{:S(2)}) collective-permute-start(f32[1,2,8,16,16]{4,0,3,2,1:T(1,128)S(1)} %bitcast.72), channel_id=1, source_target_pairs={{0,3},{1,0},{2,1},{3,2},{4,7},{5,4},{6,5},{7,6},{8,11},{9,8},{10,9... | collective-permute-start | bytes 49160 | tf_op jit(solution)/shard_map/ppermute | solution.py:50
  20.8 0.0 copy-done.1
  20.8 0.1 add_rsqrt_fusion
  21.0 0.2 copy.20
  21.2 1.8 %collective-permute-done = f32[1,2,8,16,16]{4,0,3,2,1:T(1,128)S(1)} collective-permute-done((f32[1,2,8,16,16]{4,0,3,2,1:T(1,128)S(1)}, f32[1,2,8,16,16]{4,0,3,2,1:T(1,128)S(1)}, u32[]{:S(2)}, u32[]{:S(2)}) %collective-permute-start) | collective-permute-done | bytes 16416 | tf_op jit(solution)/shard_map/ppermute | solution.py:50
  23.0 2.8 %dynamic_update_slice.9 = f32[4,2,8,16,16]{4,0,3,2,1:T(4,128)S(1)} dynamic-update-slice(f32[4,2,8,16,16]{4,0,3,2,1:T(4,128)S(1)} %bitcast.63, f32[1,2,8,16,16]{4,0,3,2,1:T(1,128)S(1)} %collective-permute-done, s32[]{:T(128)S(6)} %select_n.85, s32[]{:T(128)} %constant.104.clone.1, s32[]{:T(128)} %constant.104.clone.1, s32[]{:T(128)} %constant.104.clone.1, s32[]{:T(128)} %constant.104.clone.1) | dynamic-update-slice | bytes 32772 | tf_op jit(solution)/shard_map/dynamic_update_slice | solution.py:55
  25.8 1.8 %collective-permute-done.1 = f32[1,2,8,16,16]{4,0,3,2,1:T(1,128)S(1)} collective-permute-done((f32[1,2,8,16,16]{4,0,3,2,1:T(1,128)S(1)}, f32[1,2,8,16,16]{4,0,3,2,1:T(1,128)S(1)}, u32[]{:S(2)}, u32[]{:S(2)}) %collective-permute-start.1) | collective-permute-done | bytes 16416 | tf_op jit(solution)/shard_map/ppermute | solution.py:50
  27.6 2.8 %dynamic_update_slice.10 = f32[4,2,8,16,16]{4,0,3,2,1:T(4,128)S(1)} dynamic-update-slice(f32[4,2,8,16,16]{4,0,3,2,1:T(4,128)S(1)} %dynamic_update_slice.9, f32[1,2,8,16,16]{4,0,3,2,1:T(1,128)S(1)} %collective-permute-done.1, s32[]{:T(128)S(6)} %select_n.89, s32[]{:T(128)} %constant.104.clone.1, s32[]{:T(128)} %constant.104.clone.1, s32[]{:T(128)} %constant.104.clone.1, s32[]{:T(128)} %constant.104.clone.1) | dynamic-update-slice | bytes 32772 | tf_op jit(solution)/shard_map/dynamic_update_slice | solution.py:55
  30.4 0.0 collective-permute-done.2
  30.5 2.8 %dynamic_update_slice.11 = f32[4,2,8,16,16]{4,0,3,2,1:T(4,128)S(1)} dynamic-update-slice(f32[4,2,8,16,16]{4,0,3,2,1:T(4,128)S(1)} %dynamic_update_slice.10, f32[1,2,8,16,16]{4,0,3,2,1:T(1,128)S(1)} %collective-permute-done.2, s32[]{:T(128)S(6)} %select_n.93, s32[]{:T(128)} %constant.104.clone.1, s32[]{:T(128)} %constant.104.clone.1, s32[]{:T(128)} %constant.104.clone.1, s32[]{:T(128)} %constant.104.clone.1) | dynamic-update-slice | bytes 32772 | tf_op jit(solution)/shard_map/dynamic_update_slice | solution.py:55
  33.3 0.3 reshape.73
  33.5 0.4 convolution_multiply_fusion
  34.0 0.5 fusion.8
  34.5 0.3 copy.24
  34.7 0.2 reshape.80
  35.0 11.6 %all_to_all.54 = f32[4,1,4096]{2,1,0:T(1,128)S(1)} all-to-all(f32[4,1,4096]{2,1,0:T(1,128)S(1)} %reshape.80), channel_id=1, replica_groups=mesh['unit'=2,'row'=4,'col'=4] {'col'}, dimensions={0} | all-to-all | bytes 131072 | tf_op jit(solution)/shard_map/all_to_all | solution.py:66
  46.5 0.8 %reduce.1 = f32[4,4096]{1,0:T(4,128)S(1)} reduce(f32[4,1,4096]{2,1,0:T(1,128)S(1)} %all_to_all.54, f32[]{:T(128)} %broadcast.199), dimensions={1}, to_apply=%all_to_all.43.reduce_sub_computation | reduce | bytes 131076 | tf_op jit(solution)/shard_map/all_to_all | solution.py:66
  47.4 0.2 reshape.81
  47.6 0.3 copy.35
  47.9 0.3 all_to_all.46
  48.2 0.5 convolution_bitcast_fusion.1
  48.6 0.3 copy.26
  48.9 0.2 reshape.82
  49.2 6.5 %all_to_all.55 = f32[4,1,4096]{2,1,0:T(1,128)S(1)} all-to-all(f32[4,1,4096]{2,1,0:T(1,128)S(1)} %reshape.82), channel_id=1, replica_groups=mesh['unit'=2,'row'=4,'col'=4] {'row'}, dimensions={0} | all-to-all | bytes 131072 | tf_op jit(solution)/shard_map/all_to_all | solution.py:68
  55.6 0.8 %reduce.2 = f32[4,4096]{1,0:T(4,128)S(1)} reduce(f32[4,1,4096]{2,1,0:T(1,128)S(1)} %all_to_all.55, f32[]{:T(128)} %broadcast.199), dimensions={1}, to_apply=%all_to_all.47.reduce_sub_computation | reduce | bytes 131076 | tf_op jit(solution)/shard_map/all_to_all | solution.py:68
  56.5 0.2 reshape.83
  56.7 0.2 copy.27
  56.8 1.8 %convolution_bitcast_fusion = f32[2,32,16,16]{1,3,2,0:T(8,128)} fusion(f32[2,32,16,16]{3,2,1,0:T(8,128)S(1)} %bitcast.67, s32[32]{0:T(128)S(1)} %multiply_add_fusion.1), kind=kOutput, calls=%fused_computation | convolution fusion | flops 6306816 | bytes 131200 | tf_op jit(solution)/shard_map/dot_general | solution.py:33
  (2 shorter events, 0.0 us)
Async XLA Ops:
  0.0 1.0 %copy-start = (f32[2,32,16,16]{1,3,2,0:T(8,128)S(1)}, f32[2,32,16,16]{1,3,2,0:T(8,128)}, u32[]{:S(2)}) copy-start(f32[2,32,16,16]{1,3,2,0:T(8,128)} %param.4) | copy-start | bytes 196612
  2.8 8.4 %all-to-all-start = ((f32[4,1,4096]{2,1,0:T(1,128)}), f32[4,1,4096]{2,1,0:T(1,128)S(1)}, u32[]{:S(2)}, u32[]{:S(2)}) async-start(f32[4,1,4096]{2,1,0:T(1,128)} %reshape.78), calls=%async_computation | async-start | bytes 131072 | tf_op jit(solution)/shard_map/all_to_all | solution.py:59
  7.0 0.7 %copy-start.2 = (f32[64]{0:T(128)S(1)}, f32[64]{0:T(128)}, u32[]{:S(2)}) copy-start(f32[64]{0:T(128)} %param.6) | copy-start | bytes 772
  7.8 0.7 %copy-start.3 = (f32[32]{0:T(128)S(1)}, f32[32]{0:T(128)}, u32[]{:S(2)}) copy-start(f32[32]{0:T(128)} %param.5) | copy-start | bytes 388
  14.4 8.6 %collective-permute-start = (f32[1,2,8,16,16]{4,0,3,2,1:T(1,128)S(1)}, f32[1,2,8,16,16]{4,0,3,2,1:T(1,128)S(1)}, u32[]{:S(2)}, u32[]{:S(2)}) collective-permute-start(f32[1,2,8,16,16]{4,0,3,2,1:T(1,128)S(1)} %bitcast.74), channel_id=1, source_target_pairs={{0,1},{1,2},{2,3},{3,0},{4,5},{5,6},{6,7},{7,4},{8,9},{9,10},{10,1... | collective-permute-start | bytes 49160 | tf_op jit(solution)/shard_map/ppermute | solution.py:50
  16.6 11.0 %collective-permute-start.1 = (f32[1,2,8,16,16]{4,0,3,2,1:T(1,128)S(1)}, f32[1,2,8,16,16]{4,0,3,2,1:T(1,128)S(1)}, u32[]{:S(2)}, u32[]{:S(2)}) collective-permute-start(f32[1,2,8,16,16]{4,0,3,2,1:T(1,128)S(1)} %bitcast.73), channel_id=1, source_target_pairs={{0,2},{1,3},{2,0},{3,1},{4,6},{5,7},{6,4},{7,5},{8,10},{9,11},{10,... | collective-permute-start | bytes 49160 | tf_op jit(solution)/shard_map/ppermute | solution.py:50
  19.4 1.4 %copy-start.1 = (f32[64]{0:T(128)S(1)}, f32[64]{0:T(128)}, u32[]{:S(2)}) copy-start(f32[64]{0:T(128)} %param.7) | copy-start | bytes 772
  19.4 11.0 %collective-permute-start.2 = (f32[1,2,8,16,16]{4,0,3,2,1:T(1,128)S(1)}, f32[1,2,8,16,16]{4,0,3,2,1:T(1,128)S(1)}, u32[]{:S(2)}, u32[]{:S(2)}) collective-permute-start(f32[1,2,8,16,16]{4,0,3,2,1:T(1,128)S(1)} %bitcast.72), channel_id=1, source_target_pairs={{0,3},{1,0},{2,1},{3,2},{4,7},{5,4},{6,5},{7,6},{8,11},{9,8},{10,9... | collective-permute-start | bytes 49160 | tf_op jit(solution)/shard_map/ppermute | solution.py:50
